TPU v7x, 128 devices: a whole 4x4x4 slice. The times are simulated.
128 devices in a mesh: seq: 32 (over x, z, core), head: 4 (over y).
Axes of the slice: x: 4, y: 4, z: 4, core: 2. Of those that a mesh axis runs over, the one named last changes fastest.
Arguments:
- queries: bfloat16 [4, 4, 4, 32, 128], P(None, None, 'head', 'seq'), may hold values from -512 to 512
- key_codes: bfloat16 [4, 8, 8192, 16, 128], P(None, 'head', 'seq'), may hold values from -8 to 7, as said below
- value_codes: bfloat16 [4, 8, 8192, 16, 128], P(None, 'head', 'seq'), may hold values from -8 to 7, as said below
- key_scales: float32 [4, 8, 8192], P(None, 'head', 'seq'), may hold values from 0.05 to 0.5
- value_scales: float32 [4, 8, 8192], P(None, 'head', 'seq'), may hold values from 0.05 to 0.5
- page_ids: int32 [4, 4, 8, 4096], P(None, None, 'head', 'seq'), may hold values from 0 to 8191, as said below
- page_counts: int32 [4, 4, 8, 32], P(None, None, 'head', 'seq'), may hold values from 0 to 128, as said below
- out_weight: bfloat16 [16384, 16384], P('head', 'seq'), may hold values from -0.046875 to 0.046875
Outputs:
- projected: bfloat16 [4, 4, 16384], P(None, None, ('seq', 'head'))
Inputs may be any that keep to these rules, and one draw needn't show every extreme that they name: `page_ids`: slots r * 128 to (r + 1) * 128 - 1 name distinct pages of range r, that is pages r * 256 to (r + 1) * 256 - 1. `page_counts`: in every row of 32 counts some range has all 128 slots valid. `key_codes`: whole numbers. `value_codes`: whole numbers.
All inputs are finite; a program needn't handle non-finite values.
Results may differ from a plain program's by a relative error of at most 0.012.
The roundings to bfloat16 on the way count: a program that leaves them out, or rounds other values in their place, can miss the bound.
Values may be sent and summed in bfloat16 or wider, within the bound.
A program may use at most 128 MiB of HBM per device.

v0:
```python
import math

import jax
import jax.numpy as jnp
from jax import lax
from jax.sharding import PartitionSpec as P

NEG_FILL = -1e30


def laid_out(pieces, dim):
    pieces = jnp.moveaxis(pieces, 0, dim)
    shape = pieces.shape
    return pieces.reshape(*shape[:dim], shape[dim] * shape[dim + 1], *shape[dim + 2 :])


def sent_to_all(value, axis):
    count = lax.axis_size(axis)
    return lax.all_to_all(
        jnp.broadcast_to(value[None], (count, *value.shape)), axis, 0, 0, tiled=True
    )


def gather_directly(value, axis, dim):
    return laid_out(sent_to_all(value, axis), dim)


def in_blocks(value, dim, count):
    before, after = (value.shape[:dim], value.shape[dim + 1 :])
    return jnp.moveaxis(value.reshape(*before, count, -1, *after), dim, 0)


def sent_and_summed(value, axis, dim):
    pieces = in_blocks(value, dim, lax.axis_size(axis))
    arrived = lax.all_to_all(pieces, axis, split_axis=0, concat_axis=0, tiled=True)
    return arrived.astype(jnp.float32).sum(axis=0)


def softmax_parts(logit_scores, chosen):
    masked = jnp.where(chosen, logit_scores, NEG_FILL)
    peak_score = jnp.max(masked, axis=-1)
    weights = jnp.where(chosen, jnp.exp(masked - peak_score[..., None]), 0.0)
    weight_total = jnp.sum(weights, axis=-1)
    return (peak_score, weight_total, weights.astype(jnp.bfloat16))


def finish_merge(parts):
    stacked_out, stacked_peak, stacked_total = parts
    top_score = jnp.max(stacked_peak, axis=0)
    factor = jnp.exp(stacked_peak - top_score)
    total_all = jnp.sum(factor * stacked_total, axis=0)
    summed = jnp.sum(factor[..., None] * stacked_out, axis=0)
    return (summed / total_all[..., None]).astype(jnp.bfloat16)


def body(
    queries, key_codes, value_codes, key_scales, value_scales, page_ids, page_counts, out_weight
):
    step_count, seq_count = (queries.shape[0], queries.shape[1])
    head_dim = queries.shape[4]
    kv_local = key_codes.shape[1]
    pages_local = key_codes.shape[2]
    page_len = key_codes.shape[3]
    slot_count = page_ids.shape[3]
    gathered = gather_directly(queries, "seq", 3)
    group_size = gathered.shape[3]
    queries_per_key_head = group_size // kv_local
    query_blocks = gathered.reshape(step_count, seq_count, kv_local, queries_per_key_head, head_dim)
    local_ids = page_ids - lax.axis_index("seq") * pages_local
    live_slots = lax.broadcasted_iota(jnp.int32, (1, 1, 1, slot_count), 3) < page_counts
    inverse_sqrt_scale = 1.0 / math.sqrt(head_dim)
    key_row_block = (key_codes.astype(jnp.float32) * key_scales[..., None, None]).astype(
        jnp.bfloat16
    )
    value_rows = (value_codes.astype(jnp.float32) * value_scales[..., None, None]).astype(
        jnp.bfloat16
    )
    key_row_block = key_row_block.reshape(seq_count, kv_local, pages_local * page_len, head_dim)
    value_rows = value_rows.reshape(seq_count, kv_local, pages_local * page_len, head_dim)
    page_iota = lax.broadcasted_iota(jnp.int32, (1, 1, 1, 1, pages_local), 4)
    page_hits = jnp.any((local_ids[..., None] == page_iota) & live_slots[..., None], axis=3)
    chosen = jnp.repeat(page_hits, page_len, axis=3)[:, :, :, None, :]
    logit_scores = (
        jnp.einsum(
            "tbkqd,bknd->tbkqn", query_blocks, key_row_block, preferred_element_type=jnp.float32
        )
        * inverse_sqrt_scale
    )
    peak_score, weight_total, rounded = softmax_parts(logit_scores, chosen)
    weighted = jnp.einsum(
        "tbkqn,bknd->tbkqd", rounded, value_rows, preferred_element_type=jnp.float32
    )
    weighted = weighted.reshape(step_count, seq_count, group_size, head_dim)
    peak_score = peak_score.reshape(step_count, seq_count, group_size)
    weight_total = weight_total.reshape(step_count, seq_count, group_size)
    row_count = step_count * seq_count
    owned_heads = finish_merge(
        (
            lax.all_to_all(weighted[None], "seq", split_axis=3, concat_axis=0, tiled=True),
            lax.all_to_all(peak_score[None], "seq", split_axis=3, concat_axis=0, tiled=True),
            lax.all_to_all(weight_total[None], "seq", split_axis=3, concat_axis=0, tiled=True),
        )
    )
    piece = gather_directly(owned_heads, "seq", 2)
    head_count = piece.shape[2]
    flat_heads = piece.reshape(row_count, head_count * head_dim)
    partial_value = jnp.dot(flat_heads, out_weight, preferred_element_type=jnp.float32)
    summed = sent_and_summed(partial_value.astype(jnp.bfloat16), "head", 1)
    return summed.astype(jnp.bfloat16).reshape(step_count, seq_count, summed.shape[1])


def solution(mesh):
    placed = (
        P(None, None, "head", "seq", None),
        P(None, "head", "seq", None, None),
        P(None, "head", "seq", None, None),
        P(None, "head", "seq"),
        P(None, "head", "seq"),
        P(None, None, "head", "seq"),
        P(None, None, "head", "seq"),
        P("head", "seq"),
    )
    return jax.shard_map(
        body, mesh=mesh, in_specs=placed, out_specs=P(None, None, ("seq", "head")), check_vma=False
    )
```

profile of v0, /device:TPU:0, one launch (start us, length us, event | category | flops | bytes accessed | tf_op | source)
XLA Modules:
  0.0 115.1 jit_solution(4468347705694147972)
XLA Ops:
  0.0 1.4 %broadcast_in_dim.49 = bf16[32,4,4,1,1,128]{5,2,1,4,3,0:T(4,128)(2,1)} broadcast(bf16[4,4,128]{2,1,0:T(4,128)(2,1)} %bitcast.99), dimensions={1,2,5} | broadcast | bytes 135168 | tf_op jit(solution)/shard_map/broadcast_in_dim | solution.py:20
  1.4 8.3 %all-to-all-start = ((bf16[32,4,4,1,1,128]{5,2,1,4,3,0:T(4,128)(2,1)}), bf16[32,4,4,1,1,128]{5,2,1,4,3,0:T(4,128)(2,1)S(1)}, u32[]{:S(2)}, u32[]{:S(2)}) async-start(bf16[32,4,4,1,1,128]{5,2,1,4,3,0:T(4,128)(2,1)} %broadcast_in_dim.49), calls=%async_computation | async-start | bytes 262144 | tf_op jit(solution)/shard_map/all_to_all | solution.py:19
  9.6 0.8 copy.43
  10.4 0.1 iota_compare_fusion.1
  10.5 0.7 broadcast_subtract_fusion
  11.3 8.8 %multiply_convert_fusion.1 = bf16[4,2,256,16,128]{4,3,2,1,0:T(8,128)(2,1)} fusion(bf16[4,2,256,16,128]{4,3,2,1,0:T(8,128)(2,1)} %param.9, f32[4,2,256]{2,1,0:T(2,128)} %param.11), kind=kLoop, calls=%fused_computation.1 | loop fusion | flops 12582912 | bytes 16785408 | tf_op jit(solution)/shard_map/convert_element_type | solution.py:72
  20.1 0.0 copy-done.1
  20.1 4.6 %multiply_convert_fusion = bf16[4,2,256,16,128]{4,3,2,1,0:T(8,128)(2,1)} fusion(bf16[4,2,256,16,128]{4,3,2,1,0:T(8,128)(2,1)S(1)} %copy-done, f32[4,2,256]{2,1,0:T(2,128)S(1)} %copy-done.1), kind=kLoop, calls=%fused_computation | loop fusion | flops 12582912 | bytes 16785408 | tf_op jit(solution)/shard_map/convert_element_type | solution.py:75
  24.6 1.4 %fusion.10 = pred[4,4,2,256]{3,2,1,0:T(4,128)(4,1)S(1)} fusion(s32[4,4,2,128]{3,2,1,0:T(2,128)S(1)} %bitcast.96, pred[4,4,2,128]{3,2,1,0:T(4,128)(4,1)S(1)} %iota_compare_fusion.1), kind=kLoop, calls=%fused_computation.14 | loop fusion | flops 3137536 | bytes 28672 | tf_op jit(solution)/shard_map/reduce_or | solution.py:81
  26.1 1.4 %broadcast_in_dim.45 = pred[4,4,2,256,16]{4,3,1,2,0:T(8,128)(4,1)S(1)} broadcast(pred[4,4,2,256]{3,1,2,0:T(4,128)(4,1)S(1)} %copy.44), dimensions={0,1,2,3} | broadcast | bytes 139264 | tf_op jit(solution)/shard_map/broadcast_in_dim | solution.py:82
  27.5 2.3 %broadcast_in_dim.46 = pred[4,4,2,4096]{3,1,2,0:T(4,128)(4,1)S(1)} reshape(pred[4,4,2,256,16]{4,3,1,2,0:T(8,128)(4,1)S(1)} %broadcast_in_dim.45) | data formatting | bytes 262144 | tf_op jit(solution)/shard_map/jit(_where)/broadcast_in_dim | solution.py:40
  29.9 0.2 copy.45
  30.0 0.0 all-to-all-done
  30.1 9.6 %fusion = (f32[4,4,2,16]{3,0,2,1:T(4,128)S(1)}, f32[4,2,4096,4,16]{2,4,3,1,0:T(8,128)}) fusion(pred[4,4,2,4096]{3,0,2,1:T(4,128)(4,1)S(1)} %copy.45, bf16[4,2,4096,128,1]{3,2,4,1,0:T(8,128)(2,1)} %bitcast.90, bf16[4,4,2,16,128]{4,3,2,1,0:T(8,128)(2,1)S(1)} %bitcast.93), kind=kOutput, calls=%fused_computation.4 | convolution fusion | flops 543161856 | bytes 17041408 | tf_op jit(solution)/shard_map/tbkqd,bknd->tbkqn/dot_general | solution.py:84
  39.7 0.8 copy.60
  40.5 7.4 %all-to-all-start.1 = ((f32[1,4,4,32]{2,1,0,3:T(4,128)}), f32[1,4,4,32]{2,1,0,3:T(4,128)S(1)}, u32[]{:S(2)}, u32[]{:S(2)}) async-start(f32[1,4,4,32]{2,1,0,3:T(4,128)} %bitcast.8), calls=%async_computation.1 | async-start | bytes 131072 | tf_op jit(solution)/shard_map/all_to_all | solution.py:100
  47.9 8.0 %fusion.12 = f32[4,4,2,16,128]{4,3,0,2,1:T(8,128)S(1)} fusion(bf16[4,2,4096,128,1]{3,2,4,1,0:T(8,128)(2,1)} %bitcast.91, f32[4,2,4096,4,16]{2,4,3,1,0:T(8,128)} %get-tuple-element.6, f32[4,4,2,16]{3,0,2,1:T(4,128)S(1)} %get-tuple-element.5, pred[4,4,2,4096]{3,0,2,1:T(4,128)(4,1)S(1)} %copy.45), kind=kOutput, calls=%fused_computation.16 | convolution fusion | flops 547356672 | bytes 17172480 | tf_op jit(solution)/shard_map/tbkqn,bknd->tbkqd/dot_general | solution.py:90
  55.9 5.1 %fusion.1 = f32[4,4,2,16]{3,0,2,1:T(4,128)S(1)} fusion(f32[4,2,4096,4,16]{2,4,3,1,0:T(8,128)} %get-tuple-element.6, f32[4,4,2,16]{3,0,2,1:T(4,128)S(1)} %get-tuple-element.5, pred[4,4,2,4096]{3,0,2,1:T(4,128)(4,1)S(1)} %copy.45), kind=kLoop, calls=%fused_computation.5 | loop fusion | flops 10485248 | bytes 8523776 | tf_op jit(solution)/shard_map/reduce_sum | solution.py:43
  61.0 0.7 copy.61
  61.7 0.9 copy.51
  62.6 0.0 all-to-all-done.1
  62.6 7.4 %all-to-all-start.3 = ((f32[1,4,4,32]{2,1,0,3:T(4,128)}), f32[1,4,4,32]{2,1,0,3:T(4,128)S(1)}, u32[]{:S(2)}, u32[]{:S(2)}) async-start(f32[1,4,4,32]{2,1,0,3:T(4,128)} %bitcast.22), calls=%async_computation.3 | async-start | bytes 131072 | tf_op jit(solution)/shard_map/all_to_all | solution.py:101
  70.0 7.5 %all-to-all-done.3 = f32[1,4,4,32]{2,1,0,3:T(4,128)S(1)} async-done(((f32[1,4,4,32]{2,1,0,3:T(4,128)}), f32[1,4,4,32]{2,1,0,3:T(4,128)S(1)}, u32[]{:S(2)}, u32[]{:S(2)}) %all-to-all-start.3) | async-done | bytes 2080 | tf_op jit(solution)/shard_map/all_to_all | solution.py:101
  77.5 3.9 %all-to-all-start.2 = ((f32[1,4,4,32,128]{4,2,1,0,3:T(4,128)}), f32[1,4,4,32,128]{4,2,1,0,3:T(4,128)S(1)}, u32[]{:S(2)}, u32[]{:S(2)}) async-start(f32[1,4,4,32,128]{4,2,1,0,3:T(4,128)} %copy.51), calls=%async_computation.2 | async-start | bytes 524288 | tf_op jit(solution)/shard_map/all_to_all | solution.py:99
  81.4 0.1 fusion.21
  81.5 8.8 %all-to-all-done.2 = f32[1,4,4,32,128]{4,2,1,0,3:T(4,128)S(1)} async-done(((f32[1,4,4,32,128]{4,2,1,0,3:T(4,128)}), f32[1,4,4,32,128]{4,2,1,0,3:T(4,128)S(1)}, u32[]{:S(2)}, u32[]{:S(2)}) %all-to-all-start.2) | async-done | bytes 262176 | tf_op jit(solution)/shard_map/all_to_all | solution.py:99
  90.3 0.2 fusion.16
  90.5 0.1 divide_convert_fusion
  90.6 11.4 %all_to_all.72 = bf16[32,4,4,1,128]{4,2,1,3,0:T(4,128)(2,1)S(1)} all-to-all(bf16[32,4,4,1,128]{4,2,1,3,0:T(4,128)(2,1)S(1)} %broadcast_in_dim.52), channel_id=1, replica_groups=mesh['seq'=32,'head'=4] {'seq'}, dimensions={0} | all-to-all | bytes 262144 | tf_op jit(solution)/shard_map/all_to_all | solution.py:19
  102.0 2.8 %fusion.15 = bf16[2,4,8,128]{3,2,1,0:T(8,128)(2,1)S(1)} fusion(bf16[4096,512]{1,0:T(8,128)(2,1)} %param.15, bf16[2,8,32,128]{3,2,1,0:T(8,128)(2,1)S(1)} %bitcast.94), kind=kOutput, calls=%fused_computation.18 | convolution fusion | flops 67117056 | bytes 4341760 | tf_op jit(solution)/shard_map/dot_general | solution.py:107
  104.9 9.6 %all_to_all.73 = bf16[4,16,128]{2,1,0:T(8,128)(2,1)S(1)} all-to-all(bf16[4,16,128]{2,1,0:T(8,128)(2,1)S(1)} %bitcast.97), channel_id=1, replica_groups=mesh['seq'=32,'head'=4] {'head'}, dimensions={0} | all-to-all | bytes 32768 | tf_op jit(solution)/shard_map/all_to_all | solution.py:35
  114.5 0.6 reduce_sum.42
  (11 shorter events, 0.2 us)
Async XLA Ops:
  1.4 28.7 %all-to-all-start = ((bf16[32,4,4,1,1,128]{5,2,1,4,3,0:T(4,128)(2,1)}), bf16[32,4,4,1,1,128]{5,2,1,4,3,0:T(4,128)(2,1)S(1)}, u32[]{:S(2)}, u32[]{:S(2)}) async-start(bf16[32,4,4,1,1,128]{5,2,1,4,3,0:T(4,128)(2,1)} %broadcast_in_dim.49), calls=%async_computation | async-start | bytes 262144 | tf_op jit(solution)/shard_map/all_to_all | solution.py:19
  11.3 8.8 %copy-start = (bf16[4,2,256,16,128]{4,3,2,1,0:T(8,128)(2,1)S(1)}, bf16[4,2,256,16,128]{4,3,2,1,0:T(8,128)(2,1)}, u32[]{:S(2)}) copy-start(bf16[4,2,256,16,128]{4,3,2,1,0:T(8,128)(2,1)} %param.10) | copy-start | bytes 25165828
  11.3 8.8 %copy-start.1 = (f32[4,2,256]{2,1,0:T(2,128)S(1)}, f32[4,2,256]{2,1,0:T(2,128)}, u32[]{:S(2)}) copy-start(f32[4,2,256]{2,1,0:T(2,128)} %param.12) | copy-start | bytes 24580
  40.5 22.1 %all-to-all-start.1 = ((f32[1,4,4,32]{2,1,0,3:T(4,128)}), f32[1,4,4,32]{2,1,0,3:T(4,128)S(1)}, u32[]{:S(2)}, u32[]{:S(2)}) async-start(f32[1,4,4,32]{2,1,0,3:T(4,128)} %bitcast.8), calls=%async_computation.1 | async-start | bytes 131072 | tf_op jit(solution)/shard_map/all_to_all | solution.py:100
  62.6 14.9 %all-to-all-start.3 = ((f32[1,4,4,32]{2,1,0,3:T(4,128)}), f32[1,4,4,32]{2,1,0,3:T(4,128)S(1)}, u32[]{:S(2)}, u32[]{:S(2)}) async-start(f32[1,4,4,32]{2,1,0,3:T(4,128)} %bitcast.22), calls=%async_computation.3 | async-start | bytes 131072 | tf_op jit(solution)/shard_map/all_to_all | solution.py:101
  77.5 12.8 %all-to-all-start.2 = ((f32[1,4,4,32,128]{4,2,1,0,3:T(4,128)}), f32[1,4,4,32,128]{4,2,1,0,3:T(4,128)S(1)}, u32[]{:S(2)}, u32[]{:S(2)}) async-start(f32[1,4,4,32,128]{4,2,1,0,3:T(4,128)} %copy.51), calls=%async_computation.2 | async-start | bytes 524288 | tf_op jit(solution)/shard_map/all_to_all | solution.py:99
where the time goes:
time: 116 us; the launch traced here: 115 us
  starting transfers between devices  26.9 us (23%)
  other arithmetic  21.8 us (19%)
  blocking collectives  21 us (18%)
  matrix products  20.4 us (18%)
  waiting for transfers between devices  16.3 us (14%)
  local copies, waits for them, and re-layouts  8.57 us (7%)
    all_to_all x1, blocking collectives, sent_to_all(): lax.all_to_all(jnp.broadcast_to(value[None], (count, *value.shape)), axis...  11.4 us
    dot_general x1, matrix products, body(): jnp.einsum('tbkqd,bknd->tbkqn', query_blocks, key_row_block, preferred_el...  9.64 us
    all_to_all x1, blocking collectives, sent_and_summed(): lax.all_to_all(pieces, axis, split_axis=0, concat_axis=0, tiled=True)  9.63 us
    all_to_all x1, waiting for transfers between devices, body(): lax.all_to_all(weighted[None], 'seq', split_axis=3, concat_axis=0, tiled=...  8.83 us
    convert_element_type x1, other arithmetic, body(): (key_codes.astype(jnp.float32) * key_scales[..., None, None]).astype(jnp....  8.82 us
    all_to_all x1, starting transfers between devices, sent_to_all(): lax.all_to_all(jnp.broadcast_to(value[None], (count, *value.shape)), axis...  8.28 us
    dot_general x1, matrix products, body(): jnp.einsum('tbkqn,bknd->tbkqd', rounded, value_rows, preferred_element_ty...  7.96 us
    all_to_all x1, waiting for transfers between devices, body(): lax.all_to_all(weight_total[None], 'seq', split_axis=3, concat_axis=0, ti...  7.48 us
  transfers between devices with their start and end apart: 4, of which 2 were waited for; matrix products, arithmetic and copies ran while one was open for 31% of the time, Pallas kernels for 0%

commit v1 on v0

v1 whole, which is shorter than its diff:
```python
import functools
import math

import jax
import jax.numpy as jnp
from jax import lax
from jax.experimental import pallas as pl
from jax.experimental.pallas import tpu as pltpu
from jax.sharding import PartitionSpec as P

MESH = pl.DeviceIdType.MESH
F32 = jnp.float32
BF16 = jnp.bfloat16
CHUNK = 256
PART = 4


def seq_offsets(count):
    parts = (4, 4, 2) if count == 32 else (1, 1, count)
    steps = [(i, j, k) for i in range(parts[0]) for j in range(parts[1]) for k in range(parts[2])]
    ring = lambda d, n: min(d, n - d)
    steps = sorted(steps, key=lambda o: -(4 * (ring(o[0], parts[0]) + ring(o[1], parts[1])) + o[2]))
    return parts, steps[:-1]


def seq_peers(me, count):
    parts, steps = seq_offsets(count)
    x, z, core = me // (parts[1] * parts[2]), (me // parts[2]) % parts[1], me % parts[2]
    xs = [((x + d) % parts[0]) * (parts[1] * parts[2]) for d in range(parts[0])]
    zs = [((z + d) % parts[1]) * parts[2] for d in range(parts[1])]
    cores = [(core + d) % parts[2] for d in range(parts[2])]
    return [(o, xs[o[0]] + zs[o[1]] + cores[o[2]]) for o in steps], parts, xs


def attend_kernel(
    sizes,
    q_hbm,
    k_hbm,
    v_hbm,
    ks_hbm,
    vs_hbm,
    ids_hbm,
    cnt_hbm,
    w_hbm,
    out_ref,
    k_v,
    v_v,
    w_v,
    ks_v,
    vs_v,
    ids_v,
    cnt_v,
    kt_v,
    idm,
    hits,
    bias,
    q_all,
    q_f32,
    s_buf,
    m_buf,
    o_f32,
    a_buf,
    o_send,
    o_in,
    st_send,
    st_in,
    att_all,
    h_send,
    h_in,
    local_sem,
    k_sem,
    v_sem,
    send_sem,
    recv_sem,
):
    n_seq, n_head, steps, seqs, kvl, pages, page_len, hd = sizes
    group = n_seq
    rows = group * steps
    half = rows // kvl
    positions = pages * page_len
    chunks = positions // CHUNK
    chunk_pages = CHUNK // page_len
    slots = ids_v.shape[3]
    row_count = steps * seqs
    me = lax.axis_index("seq")
    my_head = lax.axis_index("head")
    peers, parts, plane_first = seq_peers(me, n_seq)
    planes = parts[0]
    plane = n_seq // planes

    q_copy = pltpu.make_async_copy(q_hbm, q_all.at[me], local_sem.at[0])
    ids_copy = pltpu.make_async_copy(ids_hbm, ids_v, local_sem.at[1])
    cnt_copy = pltpu.make_async_copy(cnt_hbm, cnt_v, local_sem.at[2])
    ks_copy = pltpu.make_async_copy(ks_hbm, ks_v, local_sem.at[3])
    vs_copy = pltpu.make_async_copy(vs_hbm, vs_v, local_sem.at[4])
    w_copy = pltpu.make_async_copy(w_hbm, w_v, local_sem.at[5])

    def k_copy(b):
        return pltpu.make_async_copy(k_hbm.at[b], k_v.at[b], k_sem.at[b])

    def v_copy(b):
        return pltpu.make_async_copy(v_hbm.at[b], v_v.at[b], v_sem.at[b])

    for copy in (q_copy, ids_copy, cnt_copy, ks_copy, vs_copy):
        copy.start()

    barrier = pltpu.get_barrier_semaphore()

    for _, peer in peers:
        pl.semaphore_signal(barrier, inc=1, device_id={"seq": peer}, device_id_type=MESH)
    for i in range(1, n_head):
        pl.semaphore_signal(
            barrier, inc=1, device_id={"head": (my_head + i) % n_head}, device_id_type=MESH
        )
    for b in range(seqs):
        k_copy(b).start()
        v_copy(b).start()
    w_copy.start()

    def push(src, dst, which, peer, arrival=None):
        pltpu.make_async_remote_copy(
            src_ref=src,
            dst_ref=dst,
            send_sem=send_sem.at[which],
            recv_sem=recv_sem.at[which if arrival is None else arrival],
            device_id={"seq": peer},
            device_id_type=MESH,
        ).start()

    def whole(ref, which, axis, count, arrival=None):
        block = ref.at[pl.ds(0, count)]
        return pltpu.make_async_remote_copy(
            src_ref=block,
            dst_ref=block,
            send_sem=send_sem.at[which],
            recv_sem=recv_sem.at[which if arrival is None else arrival],
            device_id={axis: 0},
            device_id_type=MESH,
        )

    ids_copy.wait()
    cnt_copy.wait()
    first_page = me * pages
    slot_iota = lax.broadcasted_iota(jnp.int32, (kvl, slots), 1)
    for t in range(steps):
        for b in range(seqs):
            counts = [
                jnp.broadcast_to(cnt_v[t, k][:, b : b + 1], (1, slots)) for k in range(kvl)
            ]
            live = slot_iota < jnp.concatenate(counts, axis=0)
            local = jnp.where(live, ids_v[t, b] - first_page, -1)
            idm[pl.ds((t * seqs + b) * kvl, kvl), :] = local.astype(F32)
    by_slot = jnp.transpose(idm[...])
    page_line = lax.broadcasted_iota(jnp.int32, (slots, pages), 1).astype(F32)
    for t in range(steps):
        for b in range(seqs):
            for k in range(kvl):
                r = (t * seqs + b) * kvl + k
                column = jnp.broadcast_to(by_slot[:, r : r + 1], (slots, pages))
                found = jnp.max(jnp.where(column == page_line, 1.0, 0.0), axis=0, keepdims=True)
                for s in range(8 // steps):
                    hits[b * kvl + k, pl.ds(s * steps + t, 1), :] = found

    q_copy.wait()
    pl.semaphore_wait(barrier, n_seq - 1 + n_head - 1)
    for _, peer in peers:
        push(q_all.at[me], q_all.at[me], 0, peer)

    page_of = lax.broadcasted_iota(jnp.int32, (pages, CHUNK), 0) % chunk_pages
    spot_of = lax.broadcasted_iota(jnp.int32, (pages, CHUNK), 1) // page_len
    spread = jnp.where(page_of == spot_of, 1.0, 0.0).astype(BF16)
    chunk_id = lax.broadcasted_iota(jnp.int32, (chunks, 8, pages), 0)
    in_chunk = lax.broadcasted_iota(jnp.int32, (chunks, 8, pages), 2) // chunk_pages == chunk_id

    def expand(entry):
        stacked = jnp.where(in_chunk, jnp.broadcast_to(entry[None], (chunks, 8, pages)), 0.0)
        stacked = stacked.reshape(chunks * 8, pages).astype(BF16)
        return jnp.dot(stacked, spread, preferred_element_type=F32).reshape(chunks, 8, CHUNK)

    log2e = 1.0 / math.log(2.0)
    score_factor = log2e / math.sqrt(hd)

    for bk in range(seqs * kvl):
        bias[bk] = (expand(hits[bk]) - 1.0) * 1e30

    ks_copy.wait()
    vs_copy.wait()

    def scaled(ref, scales, b, k, c):
        lines = []
        for i in range(chunk_pages):
            p = c * chunk_pages + i
            scale = scales[b * (kvl * pages // 128) + (p // 128) * kvl + k, p % 128]
            codes = ref[b, k, pl.ds(p * page_len, page_len), :].astype(F32)
            lines.append((codes * scale).astype(BF16))
        return jnp.concatenate(lines, axis=0)

    @pl.loop(0, seqs)
    def _(b):
        k_copy(b).wait()
        for c in range(chunks):
            for k in range(kvl):
                kt_v[b, c, pl.ds(k * hd, hd), :] = jnp.transpose(scaled(k_v, ks_v, b, k, c))
        v_copy(b).wait()
        for c in range(chunks):
            for k in range(kvl):
                v_v[b, k, pl.ds(c * CHUNK, CHUNK), :] = scaled(v_v, vs_v, b, k, c)

    whole(q_all, 0, "seq", n_seq - 1).wait_recv()
    q_f32[...] = q_all[...].astype(F32).reshape(group * row_count, hd)

    row_line = lax.broadcasted_iota(jnp.int32, (rows, hd), 0)
    lane_line = lax.broadcasted_iota(jnp.int32, (rows, hd), 1)

    def packed_queries(b):
        mine = q_f32[pl.ds(b, rows, stride=seqs), :]
        return jnp.concatenate(
            [jnp.where(row_line // half == k, mine, 0.0) for k in range(kvl)], axis=1
        ).astype(BF16)

    def score_part(b, part, queries, peak):
        for i in range(PART):
            c = part * PART + i
            raw = jnp.dot(queries, kt_v[b, c], preferred_element_type=F32)
            peaks = []
            for k in range(kvl):
                mine = raw[k * half : (k + 1) * half].reshape(half // 8, 8, CHUNK)
                mine = mine * score_factor + bias[b * kvl + k, c][None]
                mine = mine.reshape(half, CHUNK)
                s_buf[b % 2, c, pl.ds(k * half, half), :] = mine
                top = mine[:, :128]
                for j in range(1, CHUNK // 128):
                    top = jnp.maximum(top, mine[:, j * 128 : (j + 1) * 128])
                peaks.append(top)
            peak = jnp.maximum(peak, jnp.concatenate(peaks, axis=0))
        return peak

    def value_part(b, part, total, acc):
        for i in range(PART):
            c = part * PART + i
            off = c * CHUNK
            weights = []
            sums = []
            for k in range(kvl):
                lines = s_buf[b % 2, c, pl.ds(k * half, half), :]
                peak = m_buf[b % 2, pl.ds(k * half, half), :]
                peak = jnp.concatenate([peak] * (CHUNK // 128), axis=1)
                weight = jnp.exp2(lines - peak)
                part_sum = weight[:, :128]
                for j in range(1, CHUNK // 128):
                    part_sum = part_sum + weight[:, j * 128 : (j + 1) * 128]
                sums.append(part_sum)
                weights.append(weight.astype(BF16))
            values = jnp.concatenate([v_v[b, k, pl.ds(off, CHUNK), :] for k in range(kvl)], axis=1)
            total = total + jnp.concatenate(sums, axis=0)
            acc = acc + jnp.dot(
                jnp.concatenate(weights, axis=0), values, preferred_element_type=F32
            )
        return total, acc

    def set_peak(b, peak):
        peak = jnp.max(peak, axis=1, keepdims=True)
        m_buf[b % 2] = jnp.broadcast_to(peak, (rows, 128))

    low = jnp.full((rows, 128), -2e30, F32)
    first = packed_queries(0)
    peak = low
    for part in range(chunks // PART):
        peak = score_part(0, part, first, peak)
    set_peak(0, peak)
    for b in range(seqs):
        if b + 1 < seqs:
            queries = packed_queries(b + 1)

        peak = low
        total = jnp.zeros((rows, 128), F32)
        acc = jnp.zeros((rows, kvl * hd), F32)
        for part in range(chunks // PART):
            if b + 1 < seqs:
                peak = score_part(b + 1, part, queries, peak)
            total, acc = value_part(b, part, total, acc)
        total = jnp.broadcast_to(jnp.sum(total, axis=1, keepdims=True), (rows, 128))
        mine = jnp.concatenate(
            [acc[k * half : (k + 1) * half, k * hd : (k + 1) * hd] for k in range(kvl)], axis=0
        )
        o_f32[pl.ds(b, rows, stride=seqs), :] = mine / total
        level = m_buf[b % 2] + jnp.log(total) * log2e
        here = jnp.where(lane_line == (row_line % steps) * seqs + b, level, 0.0)
        if b == 0:
            a_buf[...] = here
        else:
            a_buf[...] += here
        if b + 1 < seqs:
            set_peak(b + 1, peak)

    stats = a_buf[pl.ds(0, group, stride=steps), :]
    for t in range(1, steps):
        stats = stats + a_buf[pl.ds(t, group, stride=steps), :]
    st_send[...] = stats.reshape(group, 1, 128)
    o_send[...] = o_f32[...].reshape(group, row_count, hd).astype(BF16)
    for _, peer in peers:
        push(st_send.at[peer], st_in.at[me], 1, peer)
        push(o_send.at[peer], o_in.at[me], 2, peer)
    o_in[me] = o_send[me]
    st_in[me] = st_send[me]
    whole(st_in, 1, "seq", n_seq - 1).wait_recv()
    levels = st_in[...].reshape(group, 128)
    share = jnp.exp2(levels - jnp.max(levels, axis=0, keepdims=True))
    share = share / jnp.sum(share, axis=0, keepdims=True)
    by_row = jnp.transpose(share)[:row_count]
    whole(o_in, 2, "seq", n_seq - 1).wait_recv()
    merged = jnp.zeros((row_count, hd), F32)
    for r in range(n_seq):
        merged = merged + by_row[:, r : r + 1] * o_in[r].astype(F32)
    att_all[me] = merged.astype(BF16)
    for step, peer in peers:
        push(att_all.at[me], att_all.at[me], 3, peer, 5 + (planes - step[0]) % planes)

    w_copy.wait()
    partial = None
    for d in sorted(range(planes), key=lambda d: min(d, planes - d)):
        whole(att_all, 3, "seq", plane - (d == 0), 5 + d).wait_recv()
        first_head = plane_first[d]
        flat = jnp.concatenate([att_all[first_head + j] for j in range(plane)], axis=1)
        lines = w_v[pl.ds(pl.multiple_of(first_head * hd, plane * hd), plane * hd), :]
        term = jnp.dot(flat, lines, preferred_element_type=F32)
        partial = term if partial is None else partial + term
    width = partial.shape[1] // n_head
    for h in range(n_head):
        h_send[h] = partial[:, h * width : (h + 1) * width].astype(BF16)
    for i in range(1, n_head):
        peer = (my_head + i) % n_head
        pltpu.make_async_remote_copy(
            src_ref=h_send.at[peer],
            dst_ref=h_in.at[my_head],
            send_sem=send_sem.at[4],
            recv_sem=recv_sem.at[4],
            device_id={"head": peer},
            device_id_type=MESH,
        ).start()
    h_in[my_head] = h_send[my_head]
    for which, ref in ((0, q_all), (1, st_in), (2, o_in), (3, att_all)):
        whole(ref, which, "seq", n_seq - 1).wait_send()
    whole(h_in, 4, "head", n_head - 1).wait_recv()
    whole(h_in, 4, "head", n_head - 1).wait_send()
    summed = h_in[0].astype(F32)
    for h in range(1, n_head):
        summed = summed + h_in[h].astype(F32)
    out_ref[...] = summed.astype(BF16)


def body(
    queries, key_codes, value_codes, key_scales, value_scales, page_ids, page_counts, out_weight,
    *, n_seq, n_head
):
    steps, seqs, _, _, hd = queries.shape
    _, kvl, pages, page_len, _ = key_codes.shape
    row_count = steps * seqs
    group = n_seq
    rows = group * steps
    positions = pages * page_len
    chunks = positions // CHUNK
    columns = out_weight.shape[1]
    slots = page_ids.shape[3]
    width = columns // n_head

    def by_line(scales):
        scales = scales.reshape(seqs, kvl, pages // 128, 128)
        return jnp.transpose(scales, (0, 2, 1, 3)).reshape(-1, 128)

    any_space = pl.BlockSpec(memory_space=pltpu.HBM)
    sizes = (n_seq, n_head, steps, seqs, kvl, pages, page_len, hd)
    out = pl.pallas_call(
        functools.partial(attend_kernel, sizes),
        out_shape=jax.ShapeDtypeStruct((row_count, width), BF16),
        in_specs=[any_space] * 8,
        out_specs=pl.BlockSpec(memory_space=pltpu.VMEM),
        scratch_shapes=[
            pltpu.VMEM((seqs, kvl, positions, hd), BF16),
            pltpu.VMEM((seqs, kvl, positions, hd), BF16),
            pltpu.VMEM(out_weight.shape, BF16),
            pltpu.SMEM((seqs * kvl * pages // 128, 128), F32),
            pltpu.SMEM((seqs * kvl * pages // 128, 128), F32),
            pltpu.VMEM(page_ids.shape, jnp.int32),
            pltpu.VMEM((steps, kvl, 1, seqs), jnp.int32),
            pltpu.VMEM((seqs, chunks, kvl * hd, CHUNK), BF16),
            pltpu.VMEM((steps * seqs * kvl, slots), F32),
            pltpu.VMEM((seqs * kvl, 8, pages), F32),
            pltpu.VMEM((seqs * kvl, chunks, 8, CHUNK), F32),
            pltpu.VMEM((group, row_count, hd), BF16),
            pltpu.VMEM((group * row_count, hd), F32),
            pltpu.VMEM((2, chunks, rows, CHUNK), F32),
            pltpu.VMEM((2, rows, 128), F32),
            pltpu.VMEM((group * row_count, hd), F32),
            pltpu.VMEM((rows, 128), F32),
            pltpu.VMEM((group, row_count, hd), BF16),
            pltpu.VMEM((group, row_count, hd), BF16),
            pltpu.VMEM((group, 1, 128), F32),
            pltpu.VMEM((group, 1, 128), F32),
            pltpu.VMEM((group, row_count, hd), BF16),
            pltpu.VMEM((n_head, row_count, width), BF16),
            pltpu.VMEM((n_head, row_count, width), BF16),
            pltpu.SemaphoreType.DMA((6,)),
            pltpu.SemaphoreType.DMA((seqs,)),
            pltpu.SemaphoreType.DMA((seqs,)),
            pltpu.SemaphoreType.DMA((5,)),
            pltpu.SemaphoreType.DMA((9,)),
        ],
        compiler_params=pltpu.CompilerParams(
            collective_id=0, has_side_effects=True, vmem_limit_bytes=60 * 1024 * 1024
        ),
        name="attend",
    )(
        queries.reshape(row_count, hd),
        key_codes.reshape(seqs, kvl, positions, hd),
        value_codes.reshape(seqs, kvl, positions, hd),
        by_line(key_scales),
        by_line(value_scales),
        page_ids,
        jnp.transpose(page_counts, (0, 2, 3, 1)),
        out_weight,
    )
    return out.reshape(steps, seqs, width)


def solution(mesh):
    placed = (
        P(None, None, "head", "seq", None),
        P(None, "head", "seq", None, None),
        P(None, "head", "seq", None, None),
        P(None, "head", "seq"),
        P(None, "head", "seq"),
        P(None, None, "head", "seq"),
        P(None, None, "head", "seq"),
        P("head", "seq"),
    )
    step = functools.partial(body, n_seq=mesh.shape["seq"], n_head=mesh.shape["head"])
    return jax.shard_map(
        step, mesh=mesh, in_specs=placed, out_specs=P(None, None, ("seq", "head")), check_vma=False
    )
```

time: 116 us -> 33 us (0.28)
  Pallas kernels: 0 us -> 31.5 us
  starting transfers between devices: 26.9 us -> 0 us
  other arithmetic: 21.8 us -> 0 us
  blocking collectives: 21 us -> 0 us
  matrix products: 20.4 us -> 0 us
  waiting for transfers between devices: 16.3 us -> 0 us
  local copies, waits for them, and re-layouts: 8.57 us -> 1.28 us
    pallas_call x0 -> x1, Pallas kernels: none -> 31.5 us  [body(): pl.pallas_call(functools.partial(attend_kernel, sizes), out_shape=jax.Sha...]
    all_to_all x4 -> x0, starting transfers between devices: 26.9 us -> none  [the longest x1 8.28 us: sent_to_all(): lax.all_to_all(jnp.broadcast_to(value[None], (count, *value.shape)), axis...]
    all_to_all x2 -> x0, blocking collectives: 21 us -> none  [the longest x1 11.4 us: sent_to_all(): lax.all_to_all(jnp.broadcast_to(value[None], (count, *value.shape)), axis...]
    dot_general x3 -> x0, matrix products: 20.4 us -> none  [the longest x1 9.64 us: body(): jnp.einsum('tbkqd,bknd->tbkqn', query_blocks, key_row_block, preferred_el...]
    all_to_all x4 -> x0, waiting for transfers between devices: 16.3 us -> none  [the longest x1 8.83 us: body(): lax.all_to_all(weighted[None], 'seq', split_axis=3, concat_axis=0, tiled=...]
    convert_element_type x3 -> x0, other arithmetic: 13.5 us -> none  [the longest x1 8.82 us: body(): (key_codes.astype(jnp.float32) * key_scales[..., None, None]).astype(jnp....]
    reduce_sum x4 -> x0, other arithmetic: 5.97 us -> none  [the longest x1 5.11 us: softmax_parts(): weight_total = jnp.sum(weights, axis=-1)]
    broadcast_in_dim x5 -> x0, local copies, waits for them, and re-layouts: 5.3 us -> none  [the longest x2 2.49 us: softmax_parts(): masked = jnp.where(chosen, logit_scores, NEG_FILL)]
  transfers between devices with their start and end apart: 4 -> 0, of which waited for: 2 -> 0; matrix products, arithmetic and copies ran while one was open for 31% -> 0% of each run, Pallas kernels for 0% -> 0%
where the time goes in v1:
time: 33 us; the launch traced here: 32.8 us
  Pallas kernels  31.5 us (95%)
  local copies, waits for them, and re-layouts  1.28 us (4%)
    pallas_call x1, Pallas kernels, body(): pl.pallas_call(functools.partial(attend_kernel, sizes), out_shape=jax.Sha...  31.5 us
    unnamed x1, local copies, waits for them, and re-layouts  1.28 us

profile of v1, /device:TPU:0, one launch (start us, length us, event | category | flops | bytes accessed | tf_op | source)
XLA Modules:
  0.0 32.8 jit_solution(15789448537409024325)
XLA Ops:
  0.0 31.5 %attend.1 = bf16[16,128]{1,0:T(8,128)(2,1)} custom-call(bf16[16,128]{1,0:T(8,128)(2,1)} %bitcast.20, bf16[4,2,4096,128]{3,2,1,0:T(8,128)(2,1)} %bitcast.15, bf16[4,2,4096,128]{3,2,1,0:T(8,128)(2,1)} %bitcast.16, f32[16,128]{1,0:T(8,128)} %bitcast.18, f32[16,128]{1,0:T(8,128)} %bitcast.19, s32[4,4,2,128]{3,2,1,0:T(2,128)} %ids_hbm.1, ...), custom_call_target="tpu_custom_call" | custom-call | tf_op jit(solution)/shard_map/attend/pallas_call | solution.py:373
  31.5 1.3 %copy.12 = bf16[4,4,128]{2,1,0:T(4,128)(2,1)} copy(bf16[4,4,128]{2,1,0:T(4,128)(2,1)} %bitcast.17) | data formatting | bytes 8192

commit v2 on v1

--- a/solution.py
+++ b/solution.py
@@ -223,15 +223,10 @@
             c = part * PART + i
             raw = jnp.dot(queries, kt_v[b, c], preferred_element_type=F32)
             peaks = []
-            for k in range(kvl):
-                mine = raw[k * half : (k + 1) * half].reshape(half // 8, 8, CHUNK)
-                mine = mine * score_factor + bias[b * kvl + k, c][None]
-                mine = mine.reshape(half, CHUNK)
-                s_buf[b % 2, c, pl.ds(k * half, half), :] = mine
-                top = mine[:, :128]
-                for j in range(1, CHUNK // 128):
-                    top = jnp.maximum(top, mine[:, j * 128 : (j + 1) * 128])
-                peaks.append(top)
+            for r in range(rows // 8):
+                mine = raw[r * 8 : r * 8 + 8] * score_factor + bias[b * kvl + r * 8 // half, c]
+                s_buf[b % 2, c, pl.ds(r * 8, 8), :] = mine
+                peaks.append(jnp.maximum(mine[:, :128], mine[:, 128:]))
             peak = jnp.maximum(peak, jnp.concatenate(peaks, axis=0))
         return peak
 
@@ -241,16 +236,13 @@
             off = c * CHUNK
             weights = []
             sums = []
-            for k in range(kvl):
-                lines = s_buf[b % 2, c, pl.ds(k * half, half), :]
-                peak = m_buf[b % 2, pl.ds(k * half, half), :]
-                peak = jnp.concatenate([peak] * (CHUNK // 128), axis=1)
-                weight = jnp.exp2(lines - peak)
-                part_sum = weight[:, :128]
-                for j in range(1, CHUNK // 128):
-                    part_sum = part_sum + weight[:, j * 128 : (j + 1) * 128]
-                sums.append(part_sum)
-                weights.append(weight.astype(BF16))
+            for r in range(rows // 16):
+                lines = s_buf[b % 2, c, pl.ds(r * 16, 16), :]
+                peak = m_buf[b % 2, pl.ds(r * 16, 16), :]
+                lower = jnp.exp2(lines[:, :128] - peak)
+                upper = jnp.exp2(lines[:, 128:] - peak)
+                sums.append(lower + upper)
+                weights.append(jnp.concatenate([lower.astype(BF16), upper.astype(BF16)], axis=1))
             values = jnp.concatenate([v_v[b, k, pl.ds(off, CHUNK), :] for k in range(kvl)], axis=1)
             total = total + jnp.concatenate(sums, axis=0)
             acc = acc + jnp.dot(
@@ -273,11 +265,12 @@
             queries = packed_queries(b + 1)
 
         peak = low
+        if b + 1 < seqs:
+            for part in range(chunks // PART):
+                peak = score_part(b + 1, part, queries, peak)
         total = jnp.zeros((rows, 128), F32)
         acc = jnp.zeros((rows, kvl * hd), F32)
         for part in range(chunks // PART):
-            if b + 1 < seqs:
-                peak = score_part(b + 1, part, queries, peak)
             total, acc = value_part(b, part, total, acc)
         total = jnp.broadcast_to(jnp.sum(total, axis=1, keepdims=True), (rows, 128))
         mine = jnp.concatenate(
@@ -372,7 +365,7 @@
     sizes = (n_seq, n_head, steps, seqs, kvl, pages, page_len, hd)
     out = pl.pallas_call(
         functools.partial(attend_kernel, sizes),
-        out_shape=jax.ShapeDtypeStruct((row_count, width), BF16),
+        out_shape=pltpu.VMEM((row_count, width), BF16),
         in_specs=[any_space] * 8,
         out_specs=pl.BlockSpec(memory_space=pltpu.VMEM),
         scratch_shapes=[

time: 33 us -> 31 us (0.939)
  Pallas kernels: 31.5 us -> 30.3 us
  local copies, waits for them, and re-layouts: 1.28 us -> 0.6 us
    pallas_call x1, Pallas kernels: 31.5 us -> 30.3 us  [body(): pl.pallas_call(functools.partial(attend_kernel, sizes), out_shape=pltpu.V...]
    unnamed x1, local copies, waits for them, and re-layouts: 1.28 us -> 0.6 us
where the time goes in v2:
time: 31 us; the launch traced here: 30.9 us
  Pallas kernels  30.3 us (98%)
  local copies, waits for them, and re-layouts  0.6 us (2%)
    pallas_call x1, Pallas kernels, body(): pl.pallas_call(functools.partial(attend_kernel, sizes), out_shape=pltpu.V...  30.3 us

profile of v2, /device:TPU:0, one launch (start us, length us, event | category | flops | bytes accessed | tf_op | source)
XLA Modules:
  0.0 30.9 jit_solution(11476208570910902566)
XLA Ops:
  0.0 30.3 %attend.1 = bf16[16,128]{1,0:T(8,128)(2,1)S(1)} custom-call(bf16[16,128]{1,0:T(8,128)(2,1)} %bitcast.20, bf16[4,2,4096,128]{3,2,1,0:T(8,128)(2,1)} %bitcast.16, bf16[4,2,4096,128]{3,2,1,0:T(8,128)(2,1)} %bitcast.17, f32[16,128]{1,0:T(8,128)} %bitcast.18, f32[16,128]{1,0:T(8,128)} %bitcast.19, s32[4,4,2,128]{3,2,1,0:T(2,128)} %ids_hbm.1, ...), custom_call_target="tpu_custom_call" | custom-call | tf_op jit(solution)/shard_map/attend/pallas_call | solution.py:366
  30.3 0.6 %copy.12 = bf16[4,4,128]{2,1,0:T(4,128)(2,1)} copy(bf16[4,4,128]{2,1,0:T(4,128)(2,1)S(1)} %bitcast.15) | data formatting | bytes 8192

commit v3 on v2

--- a/solution.py
+++ b/solution.py
@@ -161,11 +161,6 @@
                 for s in range(8 // steps):
                     hits[b * kvl + k, pl.ds(s * steps + t, 1), :] = found
 
-    q_copy.wait()
-    pl.semaphore_wait(barrier, n_seq - 1 + n_head - 1)
-    for _, peer in peers:
-        push(q_all.at[me], q_all.at[me], 0, peer)
-
     page_of = lax.broadcasted_iota(jnp.int32, (pages, CHUNK), 0) % chunk_pages
     spot_of = lax.broadcasted_iota(jnp.int32, (pages, CHUNK), 1) // page_len
     spread = jnp.where(page_of == spot_of, 1.0, 0.0).astype(BF16)
@@ -182,6 +177,11 @@
 
     for bk in range(seqs * kvl):
         bias[bk] = (expand(hits[bk]) - 1.0) * 1e30
+
+    q_copy.wait()
+    pl.semaphore_wait(barrier, n_seq - 1 + n_head - 1)
+    for _, peer in peers:
+        push(q_all.at[me], q_all.at[me], 0, peer)
 
     ks_copy.wait()
     vs_copy.wait()

time: 31 us -> 30.7 us (level)
  no operation moved by 1% of the time
where the time goes in v3:
time: 30.7 us; the launch traced here: 30.6 us
  Pallas kernels  30 us (98%)
  local copies, waits for them, and re-layouts  0.6 us (2%)
    pallas_call x1, Pallas kernels, body(): pl.pallas_call(functools.partial(attend_kernel, sizes), out_shape=pltpu.V...  30 us

profile of v3, /device:TPU:0, one launch (start us, length us, event | category | flops | bytes accessed | tf_op | source)
XLA Modules:
  0.0 30.6 jit_solution(12399646058508840169)
XLA Ops:
  0.0 30.0 %attend.1 = bf16[16,128]{1,0:T(8,128)(2,1)S(1)} custom-call(bf16[16,128]{1,0:T(8,128)(2,1)} %bitcast.20, bf16[4,2,4096,128]{3,2,1,0:T(8,128)(2,1)} %bitcast.16, bf16[4,2,4096,128]{3,2,1,0:T(8,128)(2,1)} %bitcast.17, f32[16,128]{1,0:T(8,128)} %bitcast.18, f32[16,128]{1,0:T(8,128)} %bitcast.19, s32[4,4,2,128]{3,2,1,0:T(2,128)} %ids_hbm.1, ...), custom_call_target="tpu_custom_call" | custom-call | tf_op jit(solution)/shard_map/attend/pallas_call | solution.py:366
  30.0 0.6 %copy.12 = bf16[4,4,128]{2,1,0:T(4,128)(2,1)} copy(bf16[4,4,128]{2,1,0:T(4,128)(2,1)S(1)} %bitcast.15) | data formatting | bytes 8192
